TPU v7x, 32 devices: a whole 2x2x4 slice. The times are simulated.
32 devices in a mesh: seq: 8 (over z, y), head: 4 (over x, core).
Axes of the slice: x: 2, y: 2, z: 4, core: 2. Of those that a mesh axis runs over, the one named last changes fastest.
Arguments:
- layer_in: bfloat16 [4096, 2048], P('seq', 'head'), may hold values from -6 to 6
- query_weight: bfloat16 [2048, 1024], P(None, 'head'), may hold values from -0.125 to 0.125
- key_weight: bfloat16 [2048, 1024], P(None, 'head'), may hold values from -0.125 to 0.125
- value_weight: bfloat16 [2048, 1024], P(None, 'head'), may hold values from -0.125 to 0.125
- gate_weight: bfloat16 [2048, 1024], P(None, 'head'), may hold values from -0.125 to 0.125
- beta_weight: bfloat16 [2048, 8], P(None, 'head'), may hold values from -0.125 to 0.125
- decay_weight: bfloat16 [2048, 8], P(None, 'head'), may hold values from -0.125 to 0.125
- conv_weight: float32 [4, 3, 1024], P(None, None, 'head'), may hold values from -3 to 3
- decay_log: float32 [8], P('head'), as said below
- beta_bias: float32 [8], P('head'), as said below
- decay_bias: float32 [8], P('head'), may hold values from -1 to 1
- norm_gain: float32 [128], replicated, may hold values from 0.1 to 1.9
- out_weight: bfloat16 [1024, 2048], P('head'), may hold values from -0.1875 to 0.1875
Outputs:
- layer_out: bfloat16 [4096, 2048], P('seq', 'head')
Inputs may be any that keep to these rules, and one draw needn't show every extreme that they name: decay_log lies between log(0.1 / 4096) and log(0.05). beta_bias lies between log(0.5 * 128 / 4096) and 1.
All inputs are finite; a program needn't handle non-finite values.
Results may differ from a plain program's by a relative error of at most 0.0049.
Values may be sent and summed in bfloat16 or wider, within the bound.
No kernel may reach another device: no remote copies, remote signals or barrier semaphores. Data moves between devices by JAX's collectives and lax.ppermute only.
A program may use at most 128 MiB of HBM per device.

v0:
```python
import jax
import jax.numpy as jnp
from jax import lax
from jax.sharding import PartitionSpec as P

BLOCK = 128
exact_mode = lax.Precision.HIGHEST
norm_floor = 0.0001


def passed_along(value, axis, steps):
    count = lax.axis_size(axis)
    leading, last = (max(0, -steps), min(count, count - steps))
    return lax.ppermute(value, axis, [(source, source + steps) for source in range(leading, last)])


def causal_conv(values, earlier, kernel):
    reach_back = kernel.shape[0] - 1
    tokens = values.shape[0]
    extended = jnp.concatenate([earlier, values], axis=0)
    summed = kernel[0] * values
    for offset in range(1, reach_back + 1):
        summed = (
            summed + kernel[offset] * extended[reach_back - offset : reach_back - offset + tokens]
        )
    return jax.nn.silu(summed)


def unit_rows(values):
    return values * lax.rsqrt(jnp.sum(values * values, axis=-1, keepdims=True) + 1.0)


def unit_lower_inverse(system):
    length = system.shape[-1]
    row_index = lax.broadcasted_iota(jnp.int32, (length, length), 0)
    col_index = lax.broadcasted_iota(jnp.int32, (length, length), 1)
    inverse = jnp.broadcast_to(jnp.eye(length, dtype=jnp.float32), system.shape)
    width = 1
    while width < length:
        same_pair = row_index // (2 * width) == col_index // (2 * width)
        lower_half = row_index // width > col_index // width
        linking = jnp.where(same_pair & lower_half, system, 0.0)
        middle = lax.optimization_barrier(
            jnp.einsum("...rs,...st->...rt", linking, inverse, precision=exact_mode)
        )
        update = lax.optimization_barrier(
            jnp.einsum("...rs,...st->...rt", inverse, middle, precision=exact_mode)
        )
        inverse = inverse - update
        width = width * 2
    return inverse


def block_terms(queries, key_rows, values, beta_gate, log_decay):
    length = log_decay.shape[-1]
    running = jnp.cumsum(log_decay, axis=-1)
    row_index = lax.broadcasted_iota(jnp.int32, (length, length), 0)
    col_index = lax.broadcasted_iota(jnp.int32, (length, length), 1)
    within = row_index >= col_index
    before = row_index > col_index
    spread = running[..., :, None] - running[..., None, :]
    decay_matrix = jnp.where(within, jnp.exp(jnp.minimum(spread, 0.0)), 0.0)
    key_gram = jnp.einsum("...rd,...sd->...rs", key_rows, key_rows, precision=exact_mode)
    lower_part = jnp.where(before, beta_gate[..., :, None] * decay_matrix * key_gram, 0.0)
    system = lower_part + jnp.eye(length, dtype=jnp.float32)
    growth = jnp.exp(running)
    right_side = jnp.concatenate(
        [beta_gate[..., None] * values, (beta_gate * growth)[..., None] * key_rows], axis=-1
    )
    solved = jnp.einsum(
        "...rs,...se->...re", unit_lower_inverse(system), right_side, precision=exact_mode
    )
    value_dim = values.shape[-1]
    fixed_rows = solved[..., :value_dim]
    erased = solved[..., value_dim:]
    query_key = jnp.einsum("...rd,...sd->...rs", queries, key_rows, precision=exact_mode)
    mixing = jnp.where(within, decay_matrix * query_key, 0.0)
    local_out = jnp.einsum("...rs,...se->...re", mixing, fixed_rows, precision=exact_mode)
    removed = lax.optimization_barrier(
        jnp.einsum("...rs,...sd->...rd", mixing, erased, precision=exact_mode)
    )
    reader = growth[..., None] * queries - removed
    tail_decay = jnp.exp(running[..., -1:] - running)
    weighted = tail_decay[..., None] * key_rows
    key_dim = key_rows.shape[-1]
    lost_part = lax.optimization_barrier(
        jnp.einsum("...bd,...be->...de", weighted, erased, precision=exact_mode)
    )
    transit = (
        jnp.exp(running[..., -1])[..., None, None] * jnp.eye(key_dim, dtype=jnp.float32) - lost_part
    )
    carried = jnp.einsum("...bd,...be->...de", weighted, fixed_rows, precision=exact_mode)
    return (local_out, reader, transit, carried)


def compose(earlier, later_map):
    joined = jnp.einsum("...de,...ef->...df", later_map[0], earlier[0], precision=exact_mode)
    moved = (
        jnp.einsum("...de,...ef->...df", later_map[0], earlier[1], precision=exact_mode)
        + later_map[1]
    )
    return (joined, moved)


def on_device(
    layer_in,
    query_weight,
    key_weight,
    value_weight,
    gate_weight,
    beta_weight,
    decay_weight,
    conv_weight,
    decay_log,
    beta_bias,
    decay_bias,
    norm_gain,
    out_weight,
):
    tokens = layer_in.shape[0]
    head_count = beta_weight.shape[1]
    head_dim = query_weight.shape[1] // head_count
    weights = (query_weight, key_weight, value_weight, gate_weight, beta_weight, decay_weight)
    shard_piece = lax.all_gather(layer_in, "head", axis=1, tiled=True)
    query_raw, key_raw, value_raw, gate_raw, beta_raw, decay_raw = tuple(
        (jnp.dot(shard_piece, weight, preferred_element_type=jnp.float32) for weight in weights)
    )
    reach_back = conv_weight.shape[0] - 1
    channels = query_raw.shape[1]
    last_rows = jnp.concatenate(
        [
            query_raw[tokens - reach_back :],
            key_raw[tokens - reach_back :],
            value_raw[tokens - reach_back :],
        ],
        axis=1,
    )
    prior_rows = passed_along(last_rows, "seq", 1)
    mixed_query = causal_conv(query_raw, prior_rows[:, :channels], conv_weight[:, 0])
    mixed_key = causal_conv(key_raw, prior_rows[:, channels : 2 * channels], conv_weight[:, 1])
    mixed_value = causal_conv(value_raw, prior_rows[:, 2 * channels :], conv_weight[:, 2])
    queries = unit_rows(mixed_query.reshape(tokens, head_count, head_dim))
    key_rows = unit_rows(mixed_key.reshape(tokens, head_count, head_dim))
    values = mixed_value.reshape(tokens, head_count, head_dim)
    beta_gate = jax.nn.sigmoid(beta_raw + beta_bias)
    log_decay = -jnp.exp(decay_log) * jax.nn.softplus(decay_raw + decay_bias)
    blocks = tokens // BLOCK

    def arrange(array):
        return array.reshape(blocks, BLOCK, head_count, head_dim).transpose(0, 2, 1, 3)

    def arrange_gate(array):
        return array.reshape(blocks, BLOCK, head_count).transpose(0, 2, 1)

    local_out, reader, transit, carried = block_terms(
        arrange(queries),
        arrange(key_rows),
        arrange(values),
        arrange_gate(beta_gate),
        arrange_gate(log_decay),
    )
    identity = jnp.broadcast_to(
        jnp.eye(head_dim, dtype=jnp.float32), (head_count, head_dim, head_dim)
    )
    nothing = jnp.zeros((head_count, head_dim, head_dim), jnp.float32)

    def through(running_pair, block_maps):
        return (compose(running_pair, block_maps), None)

    slab_pair, unused_rest = lax.scan(through, (identity, nothing), (transit, carried))
    slab_transit, slab_state = slab_pair
    stacked = jnp.stack([slab_transit, slab_state], axis=0)[None]
    every_map = lax.all_gather(stacked, "seq", axis=0, tiled=True)
    every_transit = every_map[:, 0]
    every_state = every_map[:, 1]
    position = lax.axis_index("seq")
    order = lax.broadcasted_iota(jnp.int32, (every_transit.shape[0], 1, 1, 1), 0)
    earlier_ones = order < position
    affine = (
        jnp.where(earlier_ones, every_transit, identity[None]),
        jnp.where(earlier_ones, every_state, 0.0),
    )
    while affine[0].shape[0] > 1:
        affine = compose((affine[0][0::2], affine[1][0::2]), (affine[0][1::2], affine[1][1::2]))
    incoming = affine[1][0]

    def advance(carry_state, block_maps):
        following = (
            jnp.einsum("hde,hef->hdf", block_maps[0], carry_state, precision=exact_mode)
            + block_maps[1]
        )
        return (following, carry_state)

    unused_last, starts = lax.scan(advance, incoming, (transit, carried))
    outputs = local_out + jnp.einsum("nhrd,nhde->nhre", reader, starts, precision=exact_mode)
    head_out = outputs.transpose(0, 2, 1, 3).reshape(tokens, head_count, head_dim)
    gate_rows = gate_raw.reshape(tokens, head_count, head_dim)
    scaled = head_out * lax.rsqrt(
        jnp.mean(head_out * head_out, axis=-1, keepdims=True) + norm_floor
    )
    hidden = (
        (scaled * norm_gain * jax.nn.silu(gate_rows))
        .reshape(tokens, head_count * head_dim)
        .astype(jnp.bfloat16)
    )
    column_weight = lax.all_to_all(out_weight, "head", split_axis=1, concat_axis=0, tiled=True)
    summed = jnp.dot(
        lax.all_gather(hidden, "head", axis=1, tiled=True),
        column_weight,
        preferred_element_type=jnp.float32,
    )
    return summed.astype(jnp.bfloat16)


def solution(mesh):
    return jax.shard_map(
        on_device,
        mesh=mesh,
        in_specs=(
            P("seq", "head"),
            P(None, "head"),
            P(None, "head"),
            P(None, "head"),
            P(None, "head"),
            P(None, "head"),
            P(None, "head"),
            P(None, None, "head"),
            P("head"),
            P("head"),
            P("head"),
            P(),
            P("head", None),
        ),
        out_specs=P("seq", "head"),
        check_vma=False,
    )
```

profile of v0, /device:TPU:0, one launch (start us, length us, event | category | flops | bytes accessed | tf_op | source)
XLA Modules:
  0.0 182.9 jit_solution(447879425216133817)
XLA Ops:
  8.7 1.5 fusion.147
  10.7 23.5 %all-gather.5.cloned.1.call-done = bf16[512,2048]{1,0:T(8,128)(2,1)} async-done(((bf16[512,512]{1,0:T(8,128)(2,1)}), bf16[512,2048]{1,0:T(8,128)(2,1)}) %all-gather.5.cloned.1.call-update) | async-done | bytes 2097168 | tf_op jit(solution)/shard_map/all_gather | solution.py:124
  34.2 2.4 %fusion.135 = f32[4,2,128]{2,1,0:T(2,128)S(1)} fusion(bf16[512,2048]{1,0:T(8,128)(2,1)} %all-gather.5.cloned.1.call-done, bf16[2048,2]{0,1:T(2,128)(2,1)} %param.23, f32[2]{0:T(128)} %param.27, f32[2]{0:T(128)} %exponential_negate_fusion), kind=kOutput, calls=%fused_computation.194 | convolution fusion | flops 4202496 | bytes 2109456 | tf_op jit(solution)/shard_map/dot_general | solution.py:126
  41.7 3.6 %collective-permute-start = (f32[3,768]{1,0:T(4,128)S(1)}, f32[3,768]{1,0:T(4,128)S(1)}, u32[]{:S(2)}, u32[]{:S(2)}) collective-permute-start(f32[3,768]{1,0:T(4,128)S(1)} %pad_maximum_fusion.4), channel_id=1, source_target_pairs={{0,4},{4,8},{8,12},{12,16},{16,20},{20,24},{24,28},{1,5},{5,9},{9,... | collective-permute-start | bytes 27656 | tf_op jit(solution)/shard_map/ppermute | solution.py:14
  46.5 2.2 %fusion.146 = (f32[512,256]{1,0:T(8,128)S(1)}, f32[512,256]{1,0:T(8,128)S(1)}) fusion(f32[512,256]{1,0:T(8,128)} %copy-done.7, f32[3,256]{1,0:T(4,128)S(1)} %get-tuple-element.120, f32[256]{0:T(256)} %bitcast.193, f32[256]{0:T(256)} %bitcast.194, f32[256]{0:T(256)} %bitcast.195, f32[256]{0:T(256)} %bitcast.196), kind=kLoop, calls=%fused_computation.241 | loop fusion | flops 1966080 | bytes 1580032 | tf_op jit(solution)/shard_map/mul | solution.py:30
  63.2 1.6 fusion.145
  65.3 2.2 %fusion.27 = f32[4,2,128,256]{3,2,1,0:T(8,128)S(1)} fusion(f32[4,2,128,128]{3,2,1,0:T(8,128)} %bitcast_multiply_fusion.3, f32[4,2,128,128]{3,2,1,0:T(8,128)S(1)} %bitcast_multiply_fusion.1, f32[4,2,128,128]{3,2,1,0:T(8,128)S(1)} %sub.166, f32[4,2,128,128]{3,2,1,0:T(8,128)} %fusion.157), kind=kOutput, calls=%fused_computation.42 | convolution fusion | flops 403046400 | bytes 3145728 | tf_op jit(solution)/shard_map/...rs,...se->...re/dot_general | solution.py:70
  67.5 2.1 %fusion.81 = f32[4,2,128,128]{3,2,1,0:T(8,128)} fusion(f32[4,2,128,256]{3,2,1,0:T(8,128)S(1)} %fusion.27, f32[4,128,2,128]{3,2,1,0:T(2,128)S(1)} %reshape.141, f32[4,2,128]{2,1,0:T(2,128)S(1)} %get-tuple-element.124, f32[4,128,2]{1,2,0:T(2,128)S(1)} %bitcast.179), kind=kOutput, calls=%fused_computation.117 | convolution fusion | flops 201588736 | bytes 1581056 | tf_op jit(solution)/shard_map/...bd,...be->...de/dot_general | solution.py:92
  71.0 6.0 %while.28 = (s32[]{:T(128)}, f32[2,128,128]{2,1,0:T(8,128)S(1)}, f32[2,128,128]{2,1,0:T(8,128)S(1)}, f32[4,2,128,128]{3,2,1,0:T(8,128)S(1)}, f32[4,2,128,128]{3,2,1,0:T(8,128)}) while((s32[]{:T(128)}, f32[2,128,128]{2,1,0:T(8,128)S(1)}, f32[2,128,128]{2,1,0:T(8,128)S(1)}, f32[4,2,128,128]{3,2,1,0:T(8,128)S(1)}, ...), condition=%wide.region_4.5_spmd.clone.clone, body=%wide.region_3.4_spmd.clone.sunk.clone | while | flops 100728832 | bytes 1443410 | solution.py:170
  77.9 2.1 %mul.279 = f32[512,2,128]{2,1,0:T(2,128)} reshape(f32[512,256]{1,0:T(8,128)} %get-tuple-element.101) | data formatting | bytes 1048576 | tf_op jit(solution)/shard_map/mul | solution.py:30
  80.0 2.4 %reduce_sum.27 = f32[512,2]{1,0:T(8,128)} reduce(f32[512,2,128]{2,1,0:T(2,128)} %mul.279, f32[]{:T(128)} %constant.223.clone.1), dimensions={2}, to_apply=%region_1.2 | reduce | flops 130048 | bytes 528388 | tf_op jit(solution)/shard_map/reduce_sum | solution.py:30
  82.4 1.7 add_rsqrt_fusion.1
  85.2 2.1 %reshape.140 = f32[4,128,2,128]{3,2,1,0:T(2,128)} reshape(f32[512,256]{1,0:T(8,128)} %get-tuple-element.102) | data formatting | bytes 1048576 | tf_op jit(solution)/shard_map/reshape | solution.py:142
  87.3 2.4 %fusion.17 = f32[4,2,128,128]{3,2,1,0:T(8,128)S(1)} fusion(f32[4,128,2,128]{3,2,1,0:T(2,128)} %reshape.140, f32[4,128,2,128]{3,2,1,0:T(2,128)S(1)} %reshape.141, f32[4,128,2]{1,2,0:T(2,128)S(1)} %bitcast.181, f32[4,128,2]{1,2,0:T(2,128)S(1)} %bitcast.182, f32[4,2,128]{2,1,0:T(2,128)S(1)} %reduce_window_sum.11, pred[128,128]{1,0:T(8,128)(4,1)S(1)} %get-tuple-element.137), kind=kOutput, calls=%fused_computation.25 | convolution fusion | flops 202244096 | bytes 1601536 | tf_op jit(solution)/shard_map/...rd,...sd->...rs/dot_general | solution.py:76
  91.2 1.8 fusion.87
  92.9 35.0 %all-gather.9.cloned.1.call-done = f32[16,2,128,128]{3,2,1,0:T(8,128)} async-done(((f32[2,2,128,128]{3,2,1,0:T(8,128)}), f32[16,2,128,128]{3,2,1,0:T(8,128)}) %all-gather.9.cloned.1.call-update) | async-done | bytes 2097168 | tf_op jit(solution)/shard_map/all_gather | solution.py:173
  127.9 1.8 %fusion.25 = (f32[8,2,128,128]{3,2,1,0:T(8,128)S(1)}, f32[8,2,128,128]{3,2,1,0:T(8,128)S(1)}) fusion(f32[8,2,2,128,128]{4,3,2,1,0:T(8,128)} %bitcast.173, pred[8]{0:T(512)(128)(4,1)S(1)} %iota_compare_fusion.3, f32[128,128]{1,0:T(8,128)S(1)} %fusion.133), kind=kLoop, calls=%fused_computation.39 | loop fusion | flops 524288 | bytes 4259848 | tf_op jit(solution)/shard_map/jit(_where)/select_n | solution.py:181
  132.0 7.5 %while.27 = (s32[]{:T(128)}, f32[2,128,128]{2,1,0:T(8,128)S(1)}, f32[4,2,128,128]{3,2,1,0:T(8,128)}, f32[4,2,128,128]{3,2,1,0:T(8,128)S(1)}, f32[4,2,128,128]{3,2,1,0:T(8,128)}) while((s32[]{:T(128)}, f32[2,128,128]{2,1,0:T(8,128)S(1)}, f32[4,2,128,128]{3,2,1,0:T(8,128)}, f32[4,2,128,128]{3,2,1,0:T(8,128)S(1)}, ...), condition=%wide.region_6.7_spmd.clone, body=%wide.region_5.6_spmd.sunk.clone | while | flops 50364416 | bytes 1049673 | solution.py:194
  139.6 3.8 %multiply_reduce_fusion = (f32[4,128,2]{1,2,0:T(2,128)S(1)}, f32[4,128,2,128]{1,3,2,0:T(8,128)}) fusion(f32[4,2,128,128]{2,3,1,0:T(8,128)} %fusion.87, f32[4,2,128,128]{3,2,1,0:T(8,128)} %get-tuple-element.62, f32[4,2,128,128]{3,2,1,0:T(8,128)} %fusion.84, f32[4,128,2,128]{3,2,1,0:T(2,128)} %reshape.140, f32[4,2,128]{2,1,0:T(2,128)S(1)} %get-tuple-element.122, ...), kind=kOutput, calls=%fused_computation.93 | convolution fusion | flops 202112000 | bytes 2633728 | tf_op jit(solution)/shard_map/nhrd,nhde->nhre/dot_general | solution.py:195
  143.5 2.0 %copy.104 = f32[4,128,2,128]{3,2,1,0:T(2,128)} copy(f32[4,128,2,128]{1,3,2,0:T(8,128)} %get-tuple-element.134) | data formatting | bytes 1048576 | tf_op jit(solution)/shard_map/add | solution.py:195
  146.2 2.8 %fusion.54 = bf16[512,256]{1,0:T(8,128)(2,1)} fusion(f32[64,8,2,128]{3,2,1,0:T(2,128)S(1)} %bitcast.175, f32[64,8,2,128]{3,2,1,0:T(2,128)} %bitcast.176, f32[256]{0:T(256)S(1)} %broadcast_bitcast_fusion, bf16[512,2048]{1,0:T(8,128)(2,1)S(1)} %copy-done.2, bf16[2048,256]{1,0:T(8,128)(2,1)} %param.21), kind=kOutput, calls=%fused_computation.76 | convolution fusion | flops 537919488 | bytes 4457472 | tf_op jit(solution)/shard_map/dot_general | solution.py:126
  149.0 1.5 copy.106
  150.5 22.6 %all_to_all.19 = bf16[256,4,512]{0,2,1:T(8,128)(2,1)S(1)} all-to-all(bf16[256,4,512]{0,2,1:T(8,128)(2,1)S(1)} %bitcast.172), channel_id=1, replica_groups=mesh['seq'=8,'head'=4] {'head'}, dimensions={1} | all-to-all | bytes 2097152 | tf_op jit(solution)/shard_map/all_to_all | solution.py:206
  173.6 2.7 %convolution_convert_fusion = bf16[512,512]{1,0:T(8,128)(2,1)} fusion(bf16[512,1024]{1,0:T(8,128)(2,1)} %all-gather.7.cloned.1.call-done, bf16[1024,512]{1,0:T(8,128)(2,1)S(1)} %bitcast.174), kind=kOutput, calls=%fused_computation.17 | convolution fusion | flops 537133056 | bytes 2621440 | tf_op jit(solution)/shard_map/dot_general | solution.py:207
  (152 shorter events, 44.9 us)
Async XLA Ops:
  6.5 31.6 %copy-start = (bf16[2048,256]{1,0:T(8,128)(2,1)S(1)}, bf16[2048,256]{1,0:T(8,128)(2,1)}, u32[]{:S(2)}) copy-start(bf16[2048,256]{1,0:T(8,128)(2,1)} %param.20) | copy-start | bytes 3145732
  6.5 27.7 %all-gather.5.cloned.1.call-start = ((), (), s32[]{:S(2)}) async-start(), calls=%async_computation.1 | async-start | bytes 2621440 | tf_op jit(solution)/shard_map/all_gather | solution.py:124
  7.3 120.7 %all-gather.9.cloned.1.call-start = ((), (), s32[]{:S(2)}) async-start(), calls=%async_computation.3 | async-start | bytes 2359296 | tf_op jit(solution)/shard_map/all_gather | solution.py:173
  34.2 3.9 %copy-start.1 = (bf16[512,2048]{1,0:T(8,128)(2,1)S(1)}, bf16[512,2048]{1,0:T(8,128)(2,1)}, u32[]{:S(2)}) copy-start(bf16[512,2048]{1,0:T(8,128)(2,1)} %all-gather.5.cloned.1.call-done) | copy-start | bytes 6291460
  38.2 1.2 copy-start.16
  38.9 2.8 %copy-start.3 = (f32[512,256]{1,0:T(8,128)}, f32[512,256]{1,0:T(8,128)S(1)}, u32[]{:S(2)}) copy-start(f32[512,256]{1,0:T(8,128)S(1)} %fusion.152) | copy-start | bytes 1572868
  38.9 2.0 %copy-start.17 = (bf16[2048,256]{1,0:T(8,128)(2,1)S(1)}, bf16[2048,256]{1,0:T(8,128)(2,1)}, u32[]{:S(2)}) copy-start(bf16[2048,256]{1,0:T(8,128)(2,1)} %param.18) | copy-start | bytes 3145732
  40.1 0.8 copy-start.7
  40.9 4.3 %copy-start.8 = (bf16[2048,2]{0,1:T(2,128)(2,1)S(1)}, bf16[2048,2]{0,1:T(2,128)(2,1)}, u32[]{:S(2)}) copy-start(bf16[2048,2]{0,1:T(2,128)(2,1)} %param.22) | copy-start | bytes 24580
  40.9 4.4 %copy-start.15 = (f32[2]{0:T(128)S(1)}, f32[2]{0:T(128)}, u32[]{:S(2)}) copy-start(f32[2]{0:T(128)} %param.26) | copy-start | bytes 28
  41.7 4.3 %copy-start.5 = (f32[512,256]{1,0:T(8,128)}, f32[512,256]{1,0:T(8,128)S(1)}, u32[]{:S(2)}) copy-start(f32[512,256]{1,0:T(8,128)S(1)} %fusion.150) | copy-start | bytes 1572868
  41.7 4.8 %collective-permute-start = (f32[3,768]{1,0:T(4,128)S(1)}, f32[3,768]{1,0:T(4,128)S(1)}, u32[]{:S(2)}, u32[]{:S(2)}) collective-permute-start(f32[3,768]{1,0:T(4,128)S(1)} %pad_maximum_fusion.4), channel_id=1, source_target_pairs={{0,4},{4,8},{8,12},{12,16},{16,20},{20,24},{24,28},{1,5},{5,9},{9,... | collective-permute-start | bytes 27656 | tf_op jit(solution)/shard_map/ppermute | solution.py:14
  59.6 3.5 %copy-start.4 = (f32[512,256]{1,0:T(8,128)S(1)}, f32[512,256]{1,0:T(8,128)}, u32[]{:S(2)}) copy-start(f32[512,256]{1,0:T(8,128)} %copy-done.3) | copy-start | bytes 1572868
  59.6 3.5 %copy-start.6 = (f32[512,256]{1,0:T(8,128)S(1)}, f32[512,256]{1,0:T(8,128)}, u32[]{:S(2)}) copy-start(f32[512,256]{1,0:T(8,128)} %copy-done.5) | copy-start | bytes 1572868
  59.6 3.5 %copy-start.9 = (f32[1,1,256]{2,0,1:T(1,128)S(1)}, f32[1,1,256]{2,0,1:T(1,128)}, u32[]{:S(2)}) copy-start(f32[1,1,256]{2,0,1:T(1,128)} %get-tuple-element.113) | copy-start | bytes 3076
  59.6 3.5 %copy-start.10 = (f32[1,1,256]{2,0,1:T(1,128)S(1)}, f32[1,1,256]{2,0,1:T(1,128)}, u32[]{:S(2)}) copy-start(f32[1,1,256]{2,0,1:T(1,128)} %get-tuple-element.114) | copy-start | bytes 3076
  59.6 3.5 %copy-start.11 = (f32[1,1,256]{2,0,1:T(1,128)S(1)}, f32[1,1,256]{2,0,1:T(1,128)}, u32[]{:S(2)}) copy-start(f32[1,1,256]{2,0,1:T(1,128)} %get-tuple-element.115) | copy-start | bytes 3076
  59.6 3.5 %copy-start.12 = (f32[1,1,256]{2,0,1:T(1,128)S(1)}, f32[1,1,256]{2,0,1:T(1,128)}, u32[]{:S(2)}) copy-start(f32[1,1,256]{2,0,1:T(1,128)} %get-tuple-element.116) | copy-start | bytes 3076
  59.6 3.5 %copy-start.13 = (f32[1,1,256]{2,0,1:T(1,128)S(1)}, f32[1,1,256]{2,0,1:T(1,128)}, u32[]{:S(2)}) copy-start(f32[1,1,256]{2,0,1:T(1,128)} %get-tuple-element.117) | copy-start | bytes 3076
  59.6 3.5 %copy-start.14 = (f32[1,1,256]{2,0,1:T(1,128)S(1)}, f32[1,1,256]{2,0,1:T(1,128)}, u32[]{:S(2)}) copy-start(f32[1,1,256]{2,0,1:T(1,128)} %get-tuple-element.118) | copy-start | bytes 3076
  71.0 6.9 %copy-start.18 = (f32[128]{0:T(128)S(1)}, f32[128]{0:T(128)}, u32[]{:S(2)}) copy-start(f32[128]{0:T(128)} %param.28) | copy-start | bytes 1540
  77.8 95.8 %all-gather.7.cloned.1.call-start = ((), (), s32[]{:S(2)}) async-start(), calls=%async_computation.2 | async-start | bytes 1310720 | tf_op jit(solution)/shard_map/all_gather | solution.py:208
  139.5 6.6 %copy-start.2 = (bf16[512,2048]{1,0:T(8,128)(2,1)S(1)}, bf16[512,2048]{1,0:T(8,128)(2,1)}, u32[]{:S(2)}) copy-start(bf16[512,2048]{1,0:T(8,128)(2,1)} %all-gather.5.cloned.1.call-done) | copy-start | bytes 6291460
Sparse Core Ops, SparseCore 0:
  8.9 25.2 all-gather.4
  78.0 49.9 all-gather.8
  149.1 21.0 all-gather.6
where the time goes:
time: 184 us; the launch traced here: 183 us
  waiting for transfers between devices  59.6 us (32%)
  matrix products  49.9 us (27%)
  blocking collectives  22.6 us (12%)
  local copies, waits for them, and re-layouts  17.1 us (9%)
  other arithmetic  15.9 us (9%)
  between operations  13.9 us (8%)
  starting transfers between devices  3.64 us (2%)
    all_gather x1, waiting for transfers between devices, on_device(): every_map = lax.all_gather(stacked, 'seq', axis=0, tiled=True)  35 us
    all_gather x1, waiting for transfers between devices, on_device(): shard_piece = lax.all_gather(layer_in, 'head', axis=1, tiled=True)  23.5 us
    all_to_all x1, blocking collectives, on_device(): lax.all_to_all(out_weight, 'head', split_axis=1, concat_axis=0, tiled=True)  22.6 us
    dot_general x6, matrix products, on_device(): jnp.dot(shard_piece, weight, preferred_element_type=jnp.float32)  8.02 us
    dot_general x7, matrix products, compose(): jnp.einsum('...de,...ef->...df', later_map[0], earlier[1], precision=exac...  6.03 us
    dot_general x7, matrix products, unit_lower_inverse(): jnp.einsum('...rs,...st->...rt', inverse, middle, precision=exact_mode)  5.27 us
    dot_general x7, matrix products, unit_lower_inverse(): jnp.einsum('...rs,...st->...rt', linking, inverse, precision=exact_mode)  4.78 us
    dot_general x4, matrix products, advance(): jnp.einsum('hde,hef->hdf', block_maps[0], carry_state, precision=exact_mode)  4.67 us
  transfers between devices with their start and end apart: 4, of which 3 were waited for; matrix products, arithmetic and copies ran while one was open for 12% of the time, Pallas kernels for 0%

commit v1 on v0

--- a/solution.py
+++ b/solution.py
@@ -121,7 +121,7 @@
     head_count = beta_weight.shape[1]
     head_dim = query_weight.shape[1] // head_count
     weights = (query_weight, key_weight, value_weight, gate_weight, beta_weight, decay_weight)
-    shard_piece = lax.all_gather(layer_in, "head", axis=1, tiled=True)
+    shard_piece = jnp.concatenate(lax.all_gather(layer_in, axis_name="head"), axis=1)
     query_raw, key_raw, value_raw, gate_raw, beta_raw, decay_raw = tuple(
         (jnp.dot(shard_piece, weight, preferred_element_type=jnp.float32) for weight in weights)
     )

time: 184 us -> 204 us (1.11)
  local copies, waits for them, and re-layouts: 17.1 us -> 33.1 us
  other arithmetic: 15.9 us -> 22.2 us
  waiting for transfers between devices: 59.6 us -> 54.4 us
  matrix products: 49.9 us -> 52.6 us
    all_gather x1, waiting for transfers between devices: 35 us -> 30.2 us  [on_device(): every_map = lax.all_gather(stacked, 'seq', axis=0, tiled=True)]
    reshape x0 -> x2, local copies, waits for them, and re-layouts: none -> 4.8 us  [the longest x1 2.76 us: on_device(): jnp.concatenate(lax.all_gather(layer_in, axis_name='head'), axis=1)]
    dot_general x5, matrix products: 1.73 us -> 5.35 us  [compose(): jnp.einsum('...de,...ef->...df', later_map[0], earlier[0], precision=exac...]
    all_gather x0 -> x1, local copies, waits for them, and re-layouts: none -> 3.21 us  [on_device(): lax.all_gather(layer_in, axis_name='head')]
    unnamed x41 -> x70, local copies, waits for them, and re-layouts: 4 us -> 7.1 us
    dot_general x0 -> x1, local copies, waits for them, and re-layouts: none -> 2.29 us  [on_device(): jnp.dot(shard_piece, weight, preferred_element_type=jnp.float32)]
  transfers between devices with their start and end apart: 4 -> 4, of which waited for: 3 -> 2; matrix products, arithmetic and copies ran while one was open for 12% -> 14% of each run, Pallas kernels for 0% -> 0%
where the time goes in v1:
time: 204 us; the launch traced here: 203 us
  waiting for transfers between devices  54.4 us (27%)
  matrix products  52.6 us (26%)
  local copies, waits for them, and re-layouts  33.1 us (16%)
  blocking collectives  22.6 us (11%)
  other arithmetic  22.2 us (11%)
  between operations  14 us (7%)
  starting transfers between devices  3.45 us (2%)
    all_gather x1, waiting for transfers between devices, on_device(): every_map = lax.all_gather(stacked, 'seq', axis=0, tiled=True)  30.2 us
    all_gather x1, waiting for transfers between devices, on_device(): lax.all_gather(layer_in, axis_name='head')  23.4 us
    all_to_all x1, blocking collectives, on_device(): lax.all_to_all(out_weight, 'head', split_axis=1, concat_axis=0, tiled=True)  22.6 us
    dot_general x6, matrix products, on_device(): jnp.dot(shard_piece, weight, preferred_element_type=jnp.float32)  8.01 us
    unnamed x70, local copies, waits for them, and re-layouts  7.1 us
    dot_general x7, matrix products, compose(): jnp.einsum('...de,...ef->...df', later_map[0], earlier[1], precision=exac...  6.29 us
    dot_general x5, matrix products, compose(): jnp.einsum('...de,...ef->...df', later_map[0], earlier[0], precision=exac...  5.35 us
    dot_general x7, matrix products, unit_lower_inverse(): jnp.einsum('...rs,...st->...rt', inverse, middle, precision=exact_mode)  5.27 us
  transfers between devices with their start and end apart: 4, of which 2 were waited for; matrix products, arithmetic and copies ran while one was open for 14% of the time, Pallas kernels for 0%

profile of v1, /device:TPU:0, one launch (start us, length us, event | category | flops | bytes accessed | tf_op | source)
XLA Modules:
  0.0 202.5 jit_solution(17918753465601762728)
XLA Ops:
  10.8 23.4 %all-gather.8.cloned.1.call-done = bf16[2048,512]{1,0:T(8,128)(2,1)} async-done(((bf16[512,512]{1,0:T(8,128)(2,1)}), bf16[2048,512]{1,0:T(8,128)(2,1)}) %all-gather.8.cloned.1.call-update) | async-done | bytes 2097168 | tf_op jit(solution)/shard_map/all_gather | solution.py:124
  34.2 3.2 %copy.123 = bf16[4,512,512]{2,0,1:T(4,128)(2,1)S(1)} copy(bf16[4,512,512]{2,1,0:T(8,128)(2,1)} %bitcast.174) | data formatting | bytes 4194304 | tf_op jit(solution)/shard_map/all_gather | solution.py:124
  43.2 3.4 %collective-permute-start = (f32[3,768]{1,0:T(4,128)S(1)}, f32[3,768]{1,0:T(4,128)S(1)}, u32[]{:S(2)}, u32[]{:S(2)}) collective-permute-start(f32[3,768]{1,0:T(4,128)S(1)} %pad_maximum_fusion.4), channel_id=1, source_target_pairs={{0,4},{4,8},{8,12},{12,16},{16,20},{20,24},{24,28},{1,5},{5,9},{9,... | collective-permute-start | bytes 27656 | tf_op jit(solution)/shard_map/ppermute | solution.py:14
  48.9 2.3 %fusion.147 = (f32[4,2,128]{2,1,0:T(2,128)S(1)}, f32[4,2,128]{2,1,0:T(2,128)S(1)}, f32[4,2,128]{2,1,0:T(2,128)S(1)}, f32[4,2,128]{2,1,0:T(2,128)S(1)}) fusion(f32[4,2,128]{2,1,0:T(2,128)S(1)} %reduce_window_sum.11, f32[4,2]{1,0:T(4,128)S(1)} %copy.78, f32[2]{0:T(128)S(1)} %copy-done.28, bf16[512,2048]{1,0:T(8,128)(2,1)} %bitcast.169, ...), kind=kOutput, calls=%fused_computation.242 | convolution fusion | flops 4200448 | bytes 2125864 | tf_op jit(solution)/shard_map/dot_general | solution.py:126
  51.3 3.0 %fusion.143 = (f32[512,256]{1,0:T(8,128)}, f32[512,256]{1,0:T(8,128)}) fusion(f32[512,256]{1,0:T(8,128)} %copy-done.16, f32[3,256]{1,0:T(4,128)S(1)} %get-tuple-element.122, f32[256]{0:T(256)} %bitcast.197, f32[256]{0:T(256)} %bitcast.198, f32[256]{0:T(256)} %bitcast.199, f32[256]{0:T(256)} %bitcast.200), kind=kLoop, calls=%fused_computation.238 | loop fusion | flops 1966080 | bytes 1580032 | tf_op jit(solution)/shard_map/mul | solution.py:30
  54.3 2.1 %mul.286 = f32[512,2,128]{2,1,0:T(2,128)} reshape(f32[512,256]{1,0:T(8,128)} %get-tuple-element.103) | data formatting | bytes 1048576 | tf_op jit(solution)/shard_map/mul | solution.py:30
  56.4 2.4 %reduce_sum.28 = f32[512,2]{1,0:T(8,128)} reduce(f32[512,2,128]{2,1,0:T(2,128)} %mul.286, f32[]{:T(128)} %constant.223.clone.1), dimensions={2}, to_apply=%region_2.3 | reduce | flops 130048 | bytes 528388 | tf_op jit(solution)/shard_map/reduce_sum | solution.py:30
  61.6 2.1 %reshape.148 = f32[4,128,2,128]{3,2,1,0:T(2,128)} reshape(f32[512,256]{1,0:T(8,128)} %get-tuple-element.104) | data formatting | bytes 1048576 | tf_op jit(solution)/shard_map/reshape | solution.py:143
  63.7 2.6 %fusion.16 = f32[4,2,128,128]{3,2,1,0:T(8,128)S(1)} fusion(f32[4,128,2,128]{3,2,1,0:T(2,128)} %reshape.148, f32[4,2,128]{2,1,0:T(2,128)S(1)} %get-tuple-element.134, f32[128,128]{1,0:T(8,128)S(1)} %fusion.130, f32[4,128,2]{1,2,0:T(2,128)S(1)} %bitcast.181, f32[4,2,128]{2,1,0:T(2,128)S(1)} %reduce_window_sum.11, ...), kind=kOutput, calls=%fused_computation.23 | convolution fusion | flops 202375168 | bytes 1159168 | tf_op jit(solution)/shard_map/...rd,...sd->...rs/dot_general | solution.py:63
  79.6 2.1 %reshape_reshape.3 = f32[4,128,2,128]{3,2,1,0:T(2,128)} reshape(f32[512,256]{1,0:T(8,128)} %get-tuple-element.137) | data formatting | bytes 1048576 | tf_op jit(solution)/shard_map/reshape;reshape | solution.py:150
  83.1 2.4 %fusion.27 = f32[4,2,128,256]{3,2,1,0:T(8,128)S(1)} fusion(f32[4,2,128,128]{3,2,1,0:T(8,128)} %bitcast_multiply_fusion.2, f32[4,2,128,128]{3,2,1,0:T(8,128)S(1)} %bitcast_multiply_fusion, f32[4,2,128,128]{3,2,1,0:T(8,128)} %copy-done.7, f32[4,2,128,128]{3,2,1,0:T(8,128)} %fusion.155), kind=kOutput, calls=%fused_computation.42 | convolution fusion | flops 403046400 | bytes 3145728 | tf_op jit(solution)/shard_map/...rs,...se->...re/dot_general | solution.py:70
  85.5 2.1 %fusion.78 = f32[4,2,128,128]{3,2,1,0:T(8,128)} fusion(f32[4,2,128,256]{3,2,1,0:T(8,128)S(1)} %fusion.27, f32[4,128,2,128]{3,2,1,0:T(2,128)S(1)} %copy-done.5, f32[4,2,128]{2,1,0:T(2,128)S(1)} %get-tuple-element.126, f32[4,128,2]{1,2,0:T(2,128)S(1)} %bitcast.183), kind=kOutput, calls=%fused_computation.114 | convolution fusion | flops 201588736 | bytes 1581056 | tf_op jit(solution)/shard_map/...bd,...be->...de/dot_general | solution.py:92
  89.8 9.9 %while.28 = (s32[]{:T(128)}, f32[2,128,128]{2,1,0:T(8,128)S(1)}, f32[2,128,128]{2,1,0:T(8,128)S(1)}, f32[4,2,128,128]{3,2,1,0:T(8,128)}, f32[4,2,128,128]{3,2,1,0:T(8,128)}) while((s32[]{:T(128)}, f32[2,128,128]{2,1,0:T(8,128)S(1)}, f32[2,128,128]{2,1,0:T(8,128)S(1)}, f32[4,2,128,128]{3,2,1,0:T(8,128)}, ...), condition=%wide.region_4.5_spmd.clone.clone, body=%wide.region_3.4_spmd.clone.sunk.clone | while | flops 100728832 | bytes 1443399 | solution.py:170
  100.6 2.3 %copy.90 = bf16[256,2048]{1,0:T(8,128)(2,1)} copy(bf16[256,2048]{0,1:T(8,128)(2,1)} %bitcast.177) | data formatting | bytes 2097152 | tf_op jit(solution)/shard_map/dot_general | solution.py:126
  102.9 2.8 %reshape.155 = bf16[512,2048,1]{1,0,2:T(8,128)(2,1)} reshape(bf16[512,4,512]{2,1,0:T(4,128)(2,1)S(1)} %bitcast.164) | data formatting | bytes 4194304 | tf_op jit(solution)/shard_map/reshape | solution.py:124
  105.7 2.2 %mul.269 = f32[512,2,128]{2,1,0:T(2,128)} reshape(f32[512,256]{1,0:T(8,128)} %get-tuple-element.101) | data formatting | bytes 1048576 | tf_op jit(solution)/shard_map/mul | solution.py:30
  107.8 2.5 %reduce_sum.27 = f32[512,2]{1,0:T(8,128)} reduce(f32[512,2,128]{2,1,0:T(2,128)} %mul.269, f32[]{:T(128)} %constant.223.clone.1), dimensions={2}, to_apply=%region_1.2 | reduce | flops 130048 | bytes 528388 | tf_op jit(solution)/shard_map/reduce_sum | solution.py:30
  114.2 2.4 %fusion.17 = f32[4,2,128,128]{3,2,1,0:T(8,128)S(1)} fusion(f32[4,128,2,128]{3,2,1,0:T(2,128)} %reshape.147, f32[4,128,2,128]{3,2,1,0:T(2,128)S(1)} %copy-done.6, f32[4,128,2]{1,2,0:T(2,128)S(1)} %bitcast.185, f32[4,128,2]{1,2,0:T(2,128)S(1)} %bitcast.186, f32[4,2,128]{2,1,0:T(2,128)S(1)} %reduce_window_sum.11, pred[128,128]{1,0:T(8,128)(4,1)S(1)} %get-tuple-element.139), kind=kOutput, calls=%fused_computation.25 | convolution fusion | flops 202244096 | bytes 1601536 | tf_op jit(solution)/shard_map/...rd,...sd->...rs/dot_general | solution.py:76
  118.7 30.2 %all-gather.10.cloned.1.call-done = f32[16,2,128,128]{3,2,1,0:T(8,128)} async-done(((f32[2,2,128,128]{3,2,1,0:T(8,128)}), f32[16,2,128,128]{3,2,1,0:T(8,128)}) %all-gather.10.cloned.1.call-update) | async-done | bytes 2097168 | tf_op jit(solution)/shard_map/all_gather | solution.py:173
  152.9 7.8 %while.27 = (s32[]{:T(128)}, f32[2,128,128]{2,1,0:T(8,128)S(1)}, f32[4,2,128,128]{3,2,1,0:T(8,128)}, f32[4,2,128,128]{3,2,1,0:T(8,128)}, f32[4,2,128,128]{3,2,1,0:T(8,128)}) while((s32[]{:T(128)}, f32[2,128,128]{2,1,0:T(8,128)S(1)}, f32[4,2,128,128]{3,2,1,0:T(8,128)}, f32[4,2,128,128]{3,2,1,0:T(8,128)}, ...), condition=%wide.region_6.7_spmd.clone, body=%wide.region_5.6_spmd.sunk.clone | while | flops 50364416 | bytes 1050173 | solution.py:194
  163.6 2.0 %copy.84 = f32[512,2,128]{0,2,1:T(8,128)} copy(f32[512,2,128]{2,0,1:T(8,128)} %bitcast.176) | data formatting | bytes 1048576 | tf_op jit(solution)/shard_map/reshape | solution.py:196
  165.7 2.9 %multiply_convert_fusion = bf16[512,2,128]{0,2,1:T(8,128)(2,1)} fusion(bf16[512,2048,1]{1,0,2:T(8,128)(2,1)S(1)} %copy-done.11, bf16[2,128,2048]{2,1,0:T(8,128)(2,1)} %bitcast.178, f32[512,2,128]{0,2,1:T(8,128)} %copy.84, f32[128]{0:T(128)S(1)} %copy-done.32, f32[512,2]{0,1:T(2,128)S(1)} %rsqrt_bitcast_fusion), kind=kOutput, calls=%fused_computation.89 | convolution fusion | flops 537919488 | bytes 3936768 | tf_op jit(solution)/shard_map/dot_general | solution.py:126
  170.1 22.6 %all_to_all.19 = bf16[256,4,512]{0,2,1:T(8,128)(2,1)S(1)} all-to-all(bf16[256,4,512]{0,2,1:T(8,128)(2,1)S(1)} %bitcast.173), channel_id=1, replica_groups=mesh['seq'=8,'head'=4] {'head'}, dimensions={1} | all-to-all | bytes 2097152 | tf_op jit(solution)/shard_map/all_to_all | solution.py:206
  193.2 2.8 %convolution_convert_fusion = bf16[512,512]{1,0:T(8,128)(2,1)} fusion(bf16[512,1024]{0,1:T(8,128)(2,1)} %all-gather.6.cloned.1.call-done, bf16[1024,512]{1,0:T(8,128)(2,1)S(1)} %bitcast.179), kind=kOutput, calls=%fused_computation.17 | convolution fusion | flops 537133056 | bytes 2621440 | tf_op jit(solution)/shard_map/dot_general | solution.py:207
  (182 shorter events, 64.5 us)
Async XLA Ops:
  6.5 31.5 %copy-start = (bf16[2048,256]{1,0:T(8,128)(2,1)S(1)}, bf16[2048,256]{1,0:T(8,128)(2,1)}, u32[]{:S(2)}) copy-start(bf16[2048,256]{1,0:T(8,128)(2,1)} %param.18) | copy-start | bytes 3145732
  6.5 27.7 %all-gather.8.cloned.1.call-start = ((), (), s32[]{:S(2)}) async-start(), calls=%async_computation.2 | async-start | bytes 2621440 | tf_op jit(solution)/shard_map/all_gather | solution.py:124
  7.3 141.6 %all-gather.10.cloned.1.call-start = ((), (), s32[]{:S(2)}) async-start(), calls=%async_computation.3 | async-start | bytes 2359296 | tf_op jit(solution)/shard_map/all_gather | solution.py:173
  38.1 8.5 %copy-start.1 = (bf16[64,8,4,512]{3,1,2,0:T(8,128)(2,1)}, bf16[64,8,4,512]{3,1,2,0:T(8,128)(2,1)S(1)}, u32[]{:S(2)}) copy-start(bf16[64,8,4,512]{3,1,2,0:T(8,128)(2,1)S(1)} %copy.93) | copy-start | bytes 6291460
  41.6 5.0 %copy-start.17 = (bf16[2048,2]{0,1:T(2,128)(2,1)S(1)}, bf16[2048,2]{0,1:T(2,128)(2,1)}, u32[]{:S(2)}) copy-start(bf16[2048,2]{0,1:T(2,128)(2,1)} %param.23) | copy-start | bytes 24580
  41.6 5.0 %copy-start.27 = (f32[2]{0:T(128)S(1)}, f32[2]{0:T(128)}, u32[]{:S(2)}) copy-start(f32[2]{0:T(128)} %param.27) | copy-start | bytes 28
  41.6 5.0 %copy-start.29 = (f32[2]{0:T(128)S(1)}, f32[2]{0:T(128)}, u32[]{:S(2)}) copy-start(f32[2]{0:T(128)} %exponential_negate_fusion) | copy-start | bytes 28
  41.6 7.3 %copy-start.18 = (bf16[2048,2]{0,1:T(2,128)(2,1)S(1)}, bf16[2048,2]{0,1:T(2,128)(2,1)}, u32[]{:S(2)}) copy-start(bf16[2048,2]{0,1:T(2,128)(2,1)} %param.22) | copy-start | bytes 24580
  41.6 7.3 %copy-start.28 = (f32[2]{0:T(128)S(1)}, f32[2]{0:T(128)}, u32[]{:S(2)}) copy-start(f32[2]{0:T(128)} %param.26) | copy-start | bytes 28
  43.2 8.1 %collective-permute-start = (f32[3,768]{1,0:T(4,128)S(1)}, f32[3,768]{1,0:T(4,128)S(1)}, u32[]{:S(2)}, u32[]{:S(2)}) collective-permute-start(f32[3,768]{1,0:T(4,128)S(1)} %pad_maximum_fusion.4), channel_id=1, source_target_pairs={{0,4},{4,8},{8,12},{12,16},{16,20},{20,24},{24,28},{1,5},{5,9},{9,... | collective-permute-start | bytes 27656 | tf_op jit(solution)/shard_map/ppermute | solution.py:14
  74.5 3.6 %copy-start.7 = (f32[4,2,128,128]{3,2,1,0:T(8,128)}, f32[4,2,128,128]{3,2,1,0:T(8,128)S(1)}, u32[]{:S(2)}) copy-start(f32[4,2,128,128]{3,2,1,0:T(8,128)S(1)} %sub.166) | copy-start | bytes 1572868
  74.5 3.6 %copy-start.13 = (f32[512,256]{1,0:T(8,128)S(1)}, f32[512,256]{1,0:T(8,128)}, u32[]{:S(2)}) copy-start(f32[512,256]{1,0:T(8,128)} %copy-done.12) | copy-start | bytes 1572868
  74.5 3.6 %copy-start.15 = (f32[512,256]{1,0:T(8,128)S(1)}, f32[512,256]{1,0:T(8,128)}, u32[]{:S(2)}) copy-start(f32[512,256]{1,0:T(8,128)} %copy-done.14) | copy-start | bytes 1572868
  74.5 3.6 %copy-start.19 = (f32[1,1,256]{2,0,1:T(1,128)S(1)}, f32[1,1,256]{2,0,1:T(1,128)}, u32[]{:S(2)}) copy-start(f32[1,1,256]{2,0,1:T(1,128)} %get-tuple-element.109) | copy-start | bytes 3076
  74.5 3.6 %copy-start.20 = (f32[1,1,256]{2,0,1:T(1,128)S(1)}, f32[1,1,256]{2,0,1:T(1,128)}, u32[]{:S(2)}) copy-start(f32[1,1,256]{2,0,1:T(1,128)} %get-tuple-element.110) | copy-start | bytes 3076
  81.8 3.7 %copy-start.5 = (f32[4,128,2,128]{3,2,1,0:T(2,128)S(1)}, f32[4,128,2,128]{3,2,1,0:T(2,128)}, u32[]{:S(2)}) copy-start(f32[4,128,2,128]{3,2,1,0:T(2,128)} %reshape.148) | copy-start | bytes 1572868
  85.5 4.4 %copy-start.2 = (f32[4,2,128,256]{3,2,1,0:T(8,128)}, f32[4,2,128,256]{3,2,1,0:T(8,128)S(1)}, u32[]{:S(2)}) copy-start(f32[4,2,128,256]{3,2,1,0:T(8,128)S(1)} %fusion.27) | copy-start | bytes 3145732
  100.5 92.7 %all-gather.6.cloned.1.call-start = ((), (), s32[]{:S(2)}) async-start(), calls=%async_computation.1 | async-start | bytes 1310720 | tf_op jit(solution)/shard_map/all_gather | solution.py:208
  105.6 7.5 %copy-start.9 = (f32[512,256]{1,0:T(8,128)S(1)}, f32[512,256]{1,0:T(8,128)}, u32[]{:S(2)}) copy-start(f32[512,256]{1,0:T(8,128)} %get-tuple-element.102) | copy-start | bytes 1572868
  105.6 8.5 %copy-start.6 = (f32[4,128,2,128]{3,2,1,0:T(2,128)S(1)}, f32[4,128,2,128]{3,2,1,0:T(2,128)}, u32[]{:S(2)}) copy-start(f32[4,128,2,128]{3,2,1,0:T(2,128)} %reshape.148) | copy-start | bytes 1572868
  107.8 8.7 %copy-start.3 = (f32[4,2,128,256]{3,2,1,0:T(8,128)S(1)}, f32[4,2,128,256]{3,2,1,0:T(8,128)}, u32[]{:S(2)}) copy-start(f32[4,2,128,256]{3,2,1,0:T(8,128)} %copy-done.2) | copy-start | bytes 3145732
  152.9 7.8 %copy-start.8 = (f32[4,2,128,128]{3,2,1,0:T(8,128)S(1)}, f32[4,2,128,128]{3,2,1,0:T(8,128)}, u32[]{:S(2)}) copy-start(f32[4,2,128,128]{3,2,1,0:T(8,128)} %fusion.84) | copy-start | bytes 1572868
  152.9 7.8 %copy-start.10 = (f32[4,128,2,128]{3,2,1,0:T(2,128)S(1)}, f32[4,128,2,128]{3,2,1,0:T(2,128)}, u32[]{:S(2)}) copy-start(f32[4,128,2,128]{3,2,1,0:T(2,128)} %reshape.147) | copy-start | bytes 1572868
  160.7 4.9 %copy-start.32 = (f32[128]{0:T(128)S(1)}, f32[128]{0:T(128)}, u32[]{:S(2)}) copy-start(f32[128]{0:T(128)} %param.28) | copy-start | bytes 1540
  (13 other events, 36.8 us)
Sparse Core Ops, SparseCore 0:
  8.9 25.2 all-gather.7
  100.6 48.1 all-gather.9
  168.7 20.9 all-gather.5
